TPU v7x, 32 devices: a whole 2x2x4 slice. The times are simulated.
32 devices in a mesh: grp: 2 (over y), seq: 4 (over z), head: 2 (over x), sub: 2 (over core).
Axes of the slice: x: 2, y: 2, z: 4, core: 2. Of those that a mesh axis runs over, the one named last changes fastest.
Arguments:
- latents: bfloat16 [8, 256, 1152], P(('grp', 'seq'), ('head', 'sub')), parts along dimension 0, may hold values from -6 to 6
- timestep: int32 [2], P('grp'), parts along dimension 0, may hold values from 0 to 29
- time_table: float32 [30, 3, 1152], replicated, may hold values from -3 to 3
- shift_table: float32 [2, 3, 1152], replicated, may hold values from -2 to 2
- qkv_weight: bfloat16 [2, 1152, 16, 216], P(None, None, ('head', 'sub')), may hold values from -0.1875 to 0.1875
- norm_gains: float32 [2, 2, 72], replicated, may hold values from 0.1 to 1.9
- out_weight: bfloat16 [2, 1152, 1152], P(None, ('head', 'sub')), may hold values from -0.1875 to 0.1875
Outputs:
- mixed: bfloat16 [8, 256, 1152], P(('grp', 'seq'), ('head', 'sub')), parts along dimension 0
There are 2 independent parts, one for each index of `grp`. A program takes and returns all parts, laid end to end along the dimension named above; an argument that names none is the same for every part. Nothing has to cross between parts.
All inputs are finite; a program needn't handle non-finite values.
Results may differ from a plain program's by a relative error of at most 0.0095.
Values may be sent and summed in bfloat16 or wider, within the bound.
No kernel may reach another device: no remote copies, remote signals or barrier semaphores. Data moves between devices by JAX's collectives and lax.ppermute only.
A program may use at most 64 MiB of HBM per device.

v0:
```python
import functools

import jax
import jax.numpy as jnp
from jax import lax
from jax.experimental import pallas as pl
from jax.experimental.pallas import tpu as pltpu
from jax.sharding import PartitionSpec as P

EPSILON = 1e-06
F32 = jnp.float32
BF16 = jnp.bfloat16
VMEM = pl.BlockSpec(memory_space=pltpu.VMEM)
SMEM = pl.BlockSpec(memory_space=pltpu.SMEM)
HBM = pl.BlockSpec(memory_space=pltpu.HBM)


def call(kernel, out_shape, in_specs, scratch=(), flops=0, moved=0):
    return pl.pallas_call(
        kernel,
        out_shape=out_shape,
        in_specs=in_specs,
        out_specs=jax.tree.map(lambda _: VMEM, out_shape, is_leaf=lambda leaf: hasattr(leaf, "dtype")),
        scratch_shapes=list(scratch),
        compiler_params=pltpu.CompilerParams(vmem_limit_bytes=24 * 1024 * 1024),
        cost_estimate=pl.CostEstimate(flops=flops, bytes_accessed=moved, transcendentals=0),
    )


def in_hbm(values):
    return pltpu.with_memory_space_constraint(values, pltpu.HBM)


def layer_norm(rows, shift_row, scale_row):
    wide = rows.astype(F32)
    center = jnp.mean(wide, axis=-1, keepdims=True)
    moved = wide - center
    spread = jnp.mean(moved * moved, axis=-1, keepdims=True)
    return (moved * lax.rsqrt(spread + EPSILON) * (1.0 + scale_row) + shift_row).astype(BF16)


def shuffle(values, rows, piece_rows):
    place = lax.axis_index("seq")
    count = values.shape[0]
    row = lax.broadcasted_iota(jnp.int32, (count, count), 0)
    column = lax.broadcasted_iota(jnp.int32, (count, count), 1)
    inside = row % rows
    wanted = row - inside + (place ^ (inside // piece_rows)) * piece_rows + inside % piece_rows
    return jnp.dot((wanted == column).astype(BF16), values, preferred_element_type=F32).astype(BF16)


def project(normed, weight, gain_ref, layer, heads):
    flat = lax.dot_general(weight, normed, (((1,), (1,)), ((), ())), preferred_element_type=F32)
    dim = flat.shape[0] // (3 * heads)
    pieces = []
    for head in range(heads):
        for part in range(3):
            start = (3 * head + part) * dim
            values = flat[start : start + dim]
            if part < 2:
                power = jnp.mean(values * values, axis=0, keepdims=True)
                values = values * lax.rsqrt(power + EPSILON) * gain_ref[2 * layer + part]
            pieces.append(values.astype(BF16))
    return pieces


def attend(queries, keys, values, mask):
    dim = queries.shape[0]
    scores = lax.dot_general(keys, queries, (((0,), (0,)), ((), ())), preferred_element_type=F32)
    weights = jnp.exp(scores * dim ** (-0.5))
    if mask is not None:
        weights = weights * mask
    total = jnp.sum(weights, axis=0, keepdims=True)
    mixed = jnp.dot(values, weights.astype(BF16), preferred_element_type=F32)
    return mixed / total


def first_kernel(sizes, step_ref, table_hbm, shift_hbm, own_hbm, pair_ref, norm_hbm, qkv_hbm, out_hbm,
                 mod_ref, gain_ref, packed_ref, own_ref, qkv0_ref, qkv1_ref, out0_ref, out1_ref,
                 table_ref, shift_ref, norm_ref, raw_ref, sems):
    heads, rows, piece_rows, dim = sizes
    copies = [
        pltpu.make_async_copy(source, target, sems.at[i])
        for i, (source, target) in enumerate(
            ((table_hbm, table_ref), (shift_hbm, shift_ref), (norm_hbm, norm_ref),
             (own_hbm, raw_ref), (qkv_hbm.at[0], qkv0_ref),
             (out_hbm.at[0], out0_ref), (qkv_hbm.at[1], qkv1_ref), (out_hbm.at[1], out1_ref))
        )
    ]
    for copy in copies:
        copy.start()
    for copy in copies[:4]:
        copy.wait()
    step = step_ref[0]
    for j in range(3):
        shared = table_ref[j, pl.ds(step, 1), :]
        for layer in range(2):
            mod_ref[pl.ds(3 * layer + j, 1), :] = shared + shift_ref[j, pl.ds(layer, 1), :]
    diagonal = lax.broadcasted_iota(jnp.int32, (dim, dim), 0) == lax.broadcasted_iota(jnp.int32, (dim, dim), 1)
    for layer in range(2):
        for part in range(2):
            spread = jnp.where(diagonal, norm_ref[layer, pl.ds(part, 1), :], 0.0)
            gain_ref[2 * layer + part] = jnp.sum(spread, axis=1, keepdims=True)
    own_ref[...] = shuffle(raw_ref[...], rows, piece_rows)
    tokens = jnp.concatenate([raw_ref[...], pair_ref[...]], axis=0)
    normed = layer_norm(tokens, mod_ref[pl.ds(0, 1), :], mod_ref[pl.ds(1, 1), :])
    normed = shuffle(normed, rows, piece_rows)
    copies[4].wait()
    for i, piece in enumerate(project(normed, qkv0_ref[...], gain_ref, 0, heads)):
        packed_ref[i] = piece
    for copy in copies[5:]:
        copy.wait()


def pair_kernel(heads, token_ref, gain_ref, qkv_ref, packed_ref):
    for i, piece in enumerate(project(token_ref[...], qkv_ref[...], gain_ref, 1, heads)):
        packed_ref[i] = piece


def block_kernel(sizes, *refs):
    heads, rows, piece_rows, sets, others, layer = sizes
    far = refs[:others]
    packed_ref, gain_ref, qkv_ref, out_ref = refs[others : others + 4]
    rest = refs[others + 4 :]
    tokens = jnp.concatenate([ref[...] for ref in far], axis=0) if others > 1 else far[0][...]
    if layer == 0:
        mod_ref, send_ref, keep_ref, theirs_ref = rest
        theirs_ref[...] = shuffle(far[0][...], rows, piece_rows)
        tokens = layer_norm(tokens, mod_ref[pl.ds(0, 1), :], mod_ref[pl.ds(1, 1), :])
        tokens = shuffle(tokens, rows, piece_rows)
    else:
        send_ref, keep_ref = rest
    pieces = project(tokens, qkv_ref[...], gain_ref, layer, heads)
    everything = [jnp.concatenate([packed_ref[i], pieces[i]], axis=1) for i in range(3 * heads)]
    attended = []
    if layer == 0:
        for head in range(heads):
            attended.append(attend(*everything[3 * head : 3 * head + 3], None))
    else:
        key = lax.broadcasted_iota(jnp.int32, (rows, rows), 0)
        query = lax.broadcasted_iota(jnp.int32, (rows, rows), 1)
        mask = (key % piece_rows == query % piece_rows).astype(F32)
        for head in range(heads):
            parts = []
            for start in range(0, sets * rows, rows):
                cut = [value[:, start : start + rows] for value in everything[3 * head : 3 * head + 3]]
                parts.append(attend(*cut, mask))
            attended.append(jnp.concatenate(parts, axis=1))
    stacked = jnp.concatenate(attended, axis=0).astype(BF16)
    partial = lax.dot_general(stacked, out_ref[...], (((0,), (0,)), ((), ())), preferred_element_type=F32)
    for i in range(sets // 2):
        keep_ref[i * rows : (i + 1) * rows] = partial[2 * i * rows : (2 * i + 1) * rows]
        send_ref[i * rows : (i + 1) * rows] = partial[(2 * i + 1) * rows : (2 * i + 2) * rows].astype(BF16)


def fold_kernel(keep_ref, got_ref, send_ref, kept_ref):
    half = send_ref.shape[0]
    kept_ref[...] = keep_ref[:half] + got_ref[:half].astype(F32)
    send_ref[...] = (keep_ref[half:] + got_ref[half:].astype(F32)).astype(BF16)


def split_kernel(keep_ref, got_ref, near_ref, far_ref, kept_ref):
    total = keep_ref[...] + got_ref[...].astype(F32)
    kept_ref[...] = total
    rows = total.shape[0] // 2
    half = rows // 2
    sent = total.astype(BF16)
    near_ref[...] = jnp.concatenate([sent[rows : rows + half], sent[:half]], axis=0)
    far_ref[...] = jnp.concatenate([sent[rows + half :], sent[half:rows]], axis=0)


def middle_kernel(start, piece_rows, kept_ref, got_ref, own_ref, theirs_ref, mod_ref, *refs):
    current_ref, *piece_refs = refs[-1 - own_ref.shape[0] // 2 // piece_rows :]
    rows = own_ref.shape[0]
    half = rows // 2
    total = jnp.concatenate([kept_ref[start : start + half], kept_ref[rows + start : rows + start + half]], axis=0)
    before = jnp.concatenate([own_ref[start : start + half], theirs_ref[start : start + half]], axis=0)
    update = total + got_ref[...].astype(F32)
    current = (before.astype(F32) + mod_ref[pl.ds(2, 1), :] * update).astype(BF16)
    current_ref[...] = current[:half]
    normed = layer_norm(current, mod_ref[pl.ds(3, 1), :], mod_ref[pl.ds(4, 1), :])
    for k, ref in enumerate(piece_refs):
        at = k * piece_rows
        ref[:piece_rows] = normed[at : at + piece_rows]
        ref[piece_rows:] = normed[half + at : half + at + piece_rows]


def merge_kernel(pieces, keep_ref, got_ref, send_ref, kept_ref):
    total = keep_ref[...] + got_ref[...].astype(F32)
    width = total.shape[0] // pieces
    half = width // 2
    for k in range(pieces):
        kept_ref[k * half : (k + 1) * half] = total[k * width : k * width + half]
        send_ref[k * half : (k + 1) * half] = total[k * width + half : (k + 1) * width].astype(BF16)


def finish_kernel(pieces, keep_ref, got_ref, *piece_refs):
    update = (keep_ref[...] + got_ref[...].astype(F32)).astype(BF16)
    piece_rows = update.shape[0] // pieces
    for k in range(pieces):
        piece_refs[k][...] = update[k * piece_rows : (k + 1) * piece_rows]


def last_kernel(pieces, near_ref, far_ref, mod_ref, *refs):
    update = jnp.concatenate([ref[...] for ref in refs[:pieces]], axis=0).astype(F32)
    current = jnp.concatenate([near_ref[...], far_ref[...]], axis=0).astype(F32)
    mixed = (current + mod_ref[pl.ds(5, 1), :] * update).astype(BF16)
    refs[pieces][0] = shuffle(mixed, mixed.shape[0], mixed.shape[0] // pieces)


def exchange(values, axis, count, flip):
    return lax.ppermute(values, axis, [(i, i ^ flip) for i in range(count)])


def body(head_count, sub_count, seq_count, latents, timestep, time_table, shift_table, qkv_weight, norm_gains, out_weight):
    rows, width = latents.shape[1:]
    heads, triple = qkv_weight.shape[2:]
    dim = triple // 3
    depth = out_weight.shape[1]
    blocks = head_count * sub_count
    piece_rows = rows // seq_count
    own = latents[0]
    shape = pltpu.VMEM
    flips = [1 << bit for bit in range(head_count.bit_length() - 1)]

    def spread(values, flips):
        held = {0: values}
        for place, flip in enumerate(flips):
            for j in list(held):
                held[j | 2 << place] = exchange(held[j], "head", head_count, flip)
        return held

    def reduce(send, keep, flips):
        got = exchange(send, "sub", sub_count, 1)
        for flip in reversed(flips):
            half = keep.shape[0] // 2
            send, keep = call(
                fold_kernel, (shape((half, width), BF16), shape((half, width), F32)), [VMEM] * 2, moved=half * width * 20
            )(keep, got)
            got = exchange(send, "head", head_count, flip)
        return keep, got

    def block(layer, packed, others, qkv, out, extra):
        size = others[0].shape[0]
        sets = blocks * rows // size
        half = blocks // 2 * rows
        outputs = (shape((half, width), BF16), shape((half, width), F32))
        if layer == 0:
            outputs += (shape((rows, width), BF16),)
        return call(
            functools.partial(block_kernel, (heads, size, 2 * piece_rows if layer else piece_rows, sets, len(others), layer)),
            outputs,
            [VMEM] * (len(others) + 4 + len(extra)),
            flops=2 * len(others) * size * heads * triple * width + 2 * blocks * rows * depth * width,
            moved=qkv.size * 2,
        )(*others, packed, gains, qkv, out, *extra)

    qkv = qkv_weight.transpose(0, 2, 3, 1).reshape(2, heads * triple, width)
    table = time_table.transpose(1, 0, 2)
    shift = shift_table.transpose(1, 0, 2)
    packed_shape = shape((3 * heads, dim, 2 * rows), BF16)
    work = 2 * 2 * rows * heads * triple * width

    held = spread(own, flips)
    pair = exchange(own, "sub", sub_count, 1)
    mods, gains, packed, mine, qkv0, qkv1, out0, out1 = call(
        functools.partial(first_kernel, (heads, rows, piece_rows, dim)),
        (shape((8, width), F32), shape((4, dim, 1), F32), packed_shape, shape((rows, width), BF16),
         shape(qkv.shape[1:], BF16), shape(qkv.shape[1:], BF16), shape((depth, width), BF16), shape((depth, width), BF16)),
        [SMEM, HBM, HBM, HBM, VMEM, HBM, HBM, HBM],
        [pltpu.VMEM(table.shape, F32), pltpu.VMEM(shift.shape, F32),
         pltpu.VMEM(norm_gains.shape, F32), pltpu.VMEM(own.shape, BF16), pltpu.SemaphoreType.DMA((8,))],
        flops=work,
        moved=qkv.size * 2,
    )(timestep, in_hbm(table), in_hbm(shift), in_hbm(own), pair, in_hbm(norm_gains), in_hbm(qkv), in_hbm(out_weight))

    far = [held[j] for j in sorted(held) if j]
    far, packed = lax.optimization_barrier((far, packed))
    others = [v for value in far for v in (value, exchange(value, "sub", sub_count, 1))]
    send, keep, theirs = block(0, packed, others, qkv0, out0, [mods])

    keep, got = reduce(send, keep, flips[1:])
    near, distant, kept = call(
        split_kernel,
        (shape((rows, width), BF16), shape((rows, width), BF16), shape((2 * rows, width), F32)),
        [VMEM] * 2,
        moved=rows * width * 20,
    )(keep, got)
    distant = exchange(distant, "head", head_count, 1)
    near = exchange(near, "head", head_count, 1)
    middle = seq_count // 2

    def half_block(start, got, *after):
        return call(
            functools.partial(middle_kernel, start, piece_rows),
            (shape((rows // 2, width), BF16),) + (shape((2 * piece_rows, width), BF16),) * middle,
            [VMEM] * (5 + len(after)),
            moved=rows * width * 16,
        )(kept, got, mine, theirs, mods, *after)

    current_far, *pieces_far = half_block(rows // 2, distant)
    moved = {k: exchange(pieces_far[k - middle], "seq", seq_count, k) for k in reversed(range(middle, seq_count))}
    current_near, *pieces_near = half_block(0, near, current_far)
    moved.update({k: exchange(pieces_near[k], "seq", seq_count, k) for k in reversed(range(1, middle))})
    moved[0] = pieces_near[0]
    tokens = jnp.concatenate([moved[k] for k in range(seq_count)], axis=0)

    held = spread(tokens, flips[1:])
    for j in list(held):
        held[j | 1] = exchange(held[j], "sub", sub_count, 1)
    packed = call(
        functools.partial(pair_kernel, heads), packed_shape, [VMEM] * 3, flops=work, moved=qkv.size
    )(tokens, gains, qkv1)
    send, keep = block(1, packed, [held[j] for j in sorted(held) if j], qkv1, out1, [])

    keep, got = reduce(send, keep, flips[1:])
    send, keep = call(
        functools.partial(merge_kernel, seq_count),
        (shape((rows, width), BF16), shape((rows, width), F32)),
        [VMEM] * 2,
        moved=rows * width * 20,
    )(keep, got)
    got = exchange(send, "head", head_count, 1)
    pieces = call(
        functools.partial(finish_kernel, seq_count),
        (shape((piece_rows, width), BF16),) * seq_count,
        [VMEM] * 2,
        moved=rows * width * 8,
    )(keep, got)
    back = {k: exchange(pieces[k], "seq", seq_count, k) for k in reversed(range(1, seq_count))}
    back[0] = pieces[0]
    return call(
        functools.partial(last_kernel, seq_count),
        jax.ShapeDtypeStruct((1, rows, width), BF16),
        [VMEM] * (3 + seq_count),
        moved=rows * width * 8,
    )(current_near, current_far, mods, *[back[k] for k in range(seq_count)])


def solution(mesh):
    seq_count = mesh.shape["seq"]

    def named(*args):
        return body(mesh.shape["head"], mesh.shape["sub"], seq_count, *args)

    return jax.shard_map(
        named,
        mesh=mesh,
        in_specs=(
            P(("grp", "seq"), ("head", "sub"), None),
            P("grp"),
            P(),
            P(),
            P(None, None, ("head", "sub"), None),
            P(),
            P(None, ("head", "sub"), None),
        ),
        out_specs=P(("grp", "seq"), ("head", "sub"), None),
        check_vma=False,
    )
```

profile of v0, /device:TPU:0, one launch (start us, length us, event | category | flops | bytes accessed | tf_op | source)
XLA Modules:
  0.0 52.3 jit_solution(1893545417335837674)
XLA Ops:
  0.0 0.5 collective-permute-start.1
  0.5 2.5 %collective-permute-start = (bf16[64,1152]{1,0:T(8,128)(2,1)}, bf16[64,1152]{1,0:T(8,128)(2,1)S(1)}, u32[]{:S(2)}, u32[]{:S(2)}) collective-permute-start(bf16[64,1152]{1,0:T(8,128)(2,1)} %bitcast.9), channel_id=1, source_target_pairs={{0,2},{2,0},{1,3},{3,1},{4,6},{6,4},{5,7},{7,5},{8,10},{10,8},{9,1... | collective-permute-start | bytes 442376 | tf_op jit(solution)/shard_map/ppermute | solution.py:212
  3.6 0.0 collective-permute-done.1.pair_ref
  3.6 2.8 %shard_map.73 = (f32[8,1152]{1,0:T(8,128)S(1)}, f32[4,72,1]{2,1,0:T(8,128)S(1)}, bf16[12,72,128]{2,1,0:T(8,128)(2,1)S(1)}, bf16[64,1152]{1,0:T(8,128)(2,1)S(1)},...) custom-call(s32[1]{0:T(128)S(6)} %copy.11.step_ref, ...), custom_call_target="tpu_custom_call" | custom-call | flops 254803968 | bytes 3981312 | tf_op jit(solution)/shard_map/pallas_call | solution.py:266
  6.4 1.3 %collective-permute-done.refs_0_ = bf16[64,1152]{1,0:T(8,128)(2,1)S(1)} collective-permute-done((bf16[64,1152]{1,0:T(8,128)(2,1)}, bf16[64,1152]{1,0:T(8,128)(2,1)S(1)}, u32[]{:S(2)}, u32[]{:S(2)}) %collective-permute-start) | collective-permute-done | bytes 147488 | tf_op jit(solution)/shard_map/ppermute | solution.py:212
  7.7 0.0 collective-permute-start.2
  7.7 1.4 %collective-permute-done.2.refs_1_ = bf16[64,1152]{1,0:T(8,128)(2,1)S(1)} collective-permute-done((bf16[64,1152]{1,0:T(8,128)(2,1)S(1)}, bf16[64,1152]{1,0:T(8,128)(2,1)S(1)}, u32[]{:S(2)}, u32[]{:S(2)}) %collective-permute-start.2) | collective-permute-done | bytes 147488 | tf_op jit(solution)/shard_map/ppermute | solution.py:212
  9.1 3.0 %shard_map.74 = (bf16[128,1152]{1,0:T(8,128)(2,1)S(1)}, f32[128,1152]{1,0:T(8,128)S(1)}, bf16[64,1152]{1,0:T(8,128)(2,1)S(1)}) custom-call(bf16[64,1152]{1,0:T(8,128)(2,1)S(1)} %collective-permute-done.refs_0_, bf16[64,1152]{1,0:T(8,128)(2,1)S(1)} %collective-permute-done.2.refs_1_, bf16[12,72,128]{2,1,0:T(8,128)(2,1)S(1)} %get-tuple-element.37.refs_2_, ...), custom_call_target="tpu_custom_call" | custom-call | flops 424673280 | bytes 1990656 | tf_op jit(solution)/shard_map/pallas_call | solution.py:250
  12.1 0.2 collective-permute-start.3
  12.3 1.4 %collective-permute-done.3.got_ref = bf16[128,1152]{1,0:T(8,128)(2,1)S(1)} collective-permute-done((bf16[128,1152]{1,0:T(8,128)(2,1)S(1)}, bf16[128,1152]{1,0:T(8,128)(2,1)S(1)}, u32[]{:S(2)}, u32[]{:S(2)}) %collective-permute-start.3) | collective-permute-done | bytes 294944 | tf_op jit(solution)/shard_map/ppermute | solution.py:212
  13.8 0.1 shard_map.75
  13.8 1.8 %collective-permute-start.5 = (bf16[64,1152]{1,0:T(8,128)(2,1)S(1)}, bf16[64,1152]{1,0:T(8,128)(2,1)S(1)}, u32[]{:S(2)}, u32[]{:S(2)}) collective-permute-start(bf16[64,1152]{1,0:T(8,128)(2,1)S(1)} %get-tuple-element.48), channel_id=1, source_target_pairs={{0,2},{2,0},{1,3},{3,1},{4,6},{6,4},{5,7},{7,5},{8,10},{10,8},{9,1... | collective-permute-start | bytes 442376 | tf_op jit(solution)/shard_map/ppermute | solution.py:212
  15.7 0.3 collective-permute-start.4
  15.9 4.7 %collective-permute-done.5.got_ref = bf16[64,1152]{1,0:T(8,128)(2,1)S(1)} collective-permute-done((bf16[64,1152]{1,0:T(8,128)(2,1)S(1)}, bf16[64,1152]{1,0:T(8,128)(2,1)S(1)}, u32[]{:S(2)}, u32[]{:S(2)}) %collective-permute-start.5) | collective-permute-done | bytes 147488 | tf_op jit(solution)/shard_map/ppermute | solution.py:212
  20.6 0.3 shard_map.76
  20.9 2.9 %collective-permute-start.7 = (bf16[32,1152]{1,0:T(8,128)(2,1)S(1)}, bf16[32,1152]{1,0:T(8,128)(2,1)S(1)}, u32[]{:S(2)}, u32[]{:S(2)}) collective-permute-start(bf16[32,1152]{1,0:T(8,128)(2,1)S(1)} %get-tuple-element.53), channel_id=1, source_target_pairs={{0,8},{4,12},{8,0},{12,4},{1,9},{5,13},{9,1},{13,5},{2,10},{6,14},... | collective-permute-start | bytes 221192 | tf_op jit(solution)/shard_map/ppermute | solution.py:212
  23.8 1.3 %collective-permute-start.8 = (bf16[32,1152]{1,0:T(8,128)(2,1)S(1)}, bf16[32,1152]{1,0:T(8,128)(2,1)S(1)}, u32[]{:S(2)}, u32[]{:S(2)}) collective-permute-start(bf16[32,1152]{1,0:T(8,128)(2,1)S(1)} %get-tuple-element.54), channel_id=1, source_target_pairs={{0,12},{4,8},{8,4},{12,0},{1,13},{5,9},{9,5},{13,1},{2,14},{6,10},... | collective-permute-start | bytes 221192 | tf_op jit(solution)/shard_map/ppermute | solution.py:212
  25.2 0.0 collective-permute-done.4.got_ref
  25.2 0.3 shard_map.77
  25.4 0.3 collective-permute-start.6
  25.7 4.9 %collective-permute-done.6 = bf16[32,1152]{1,0:T(8,128)(2,1)S(1)} collective-permute-done((bf16[32,1152]{1,0:T(8,128)(2,1)S(1)}, bf16[32,1152]{1,0:T(8,128)(2,1)S(1)}, u32[]{:S(2)}, u32[]{:S(2)}) %collective-permute-start.6) | collective-permute-done | bytes 73760 | tf_op jit(solution)/shard_map/ppermute | solution.py:212
  30.7 0.0 collective-permute-done.7
  30.7 0.0 collective-permute-done.8
  30.7 0.1 collective-permute-start.9
  30.8 0.7 %shard_map.78.refs_1_ = bf16[12,72,128]{2,1,0:T(8,128)(2,1)S(1)} custom-call(bf16[128,1152]{1,0:T(8,128)(2,1)S(1)} %constant_dynamic-update-slice_fusion.token_ref, f32[4,72,1]{2,1,0:T(8,128)S(1)} %get-tuple-element.38.refs_3_.gain_ref.refs_2_, bf16[864,1152]{1,0:T(8,128)(2,1)S(1)} %get-tuple-element.55.qkv_ref.refs_3_), custom_call_target="tpu_custom_call" | custom-call | flops 254803968 | bytes 1990656 | tf_op jit(solution)/shard_map/pallas_call | solution.py:311
  31.5 0.9 %collective-permute-done.9.refs_0_ = bf16[128,1152]{1,0:T(8,128)(2,1)S(1)} collective-permute-done((bf16[128,1152]{1,0:T(8,128)(2,1)S(1)}, bf16[128,1152]{1,0:T(8,128)(2,1)S(1)}, u32[]{:S(2)}, u32[]{:S(2)}) %collective-permute-start.9) | collective-permute-done | bytes 294944 | tf_op jit(solution)/shard_map/ppermute | solution.py:212
  32.4 2.9 %shard_map.79 = (bf16[128,1152]{1,0:T(8,128)(2,1)S(1)}, f32[128,1152]{1,0:T(8,128)S(1)}) custom-call(bf16[128,1152]{1,0:T(8,128)(2,1)S(1)} %collective-permute-done.9.refs_0_, bf16[12,72,128]{2,1,0:T(8,128)(2,1)S(1)} %shard_map.78.refs_1_, f32[4,72,1]{2,1,0:T(8,128)S(1)} %get-tuple-element.38.refs_3_.gain_ref.refs_2_, ...), custom_call_target="tpu_custom_call" | custom-call | flops 424673280 | bytes 1990656 | tf_op jit(solution)/shard_map/pallas_call | solution.py:250
  35.3 0.2 collective-permute-start.10
  35.5 1.4 %collective-permute-done.10.got_ref = bf16[128,1152]{1,0:T(8,128)(2,1)S(1)} collective-permute-done((bf16[128,1152]{1,0:T(8,128)(2,1)S(1)}, bf16[128,1152]{1,0:T(8,128)(2,1)S(1)}, u32[]{:S(2)}, u32[]{:S(2)}) %collective-permute-start.10) | collective-permute-done | bytes 294944 | tf_op jit(solution)/shard_map/ppermute | solution.py:212
  37.0 1.6 %collective-permute-start.11 = (bf16[64,1152]{1,0:T(8,128)(2,1)S(1)}, bf16[64,1152]{1,0:T(8,128)(2,1)S(1)}, u32[]{:S(2)}, u32[]{:S(2)}) collective-permute-start(bf16[64,1152]{1,0:T(8,128)(2,1)S(1)} %get-tuple-element.60), channel_id=1, source_target_pairs={{0,2},{2,0},{1,3},{3,1},{4,6},{6,4},{5,7},{7,5},{8,10},{10,8},{9,1... | collective-permute-start | bytes 442376 | tf_op jit(solution)/shard_map/ppermute | solution.py:212
  38.5 4.4 %collective-permute-done.11.got_ref = bf16[64,1152]{1,0:T(8,128)(2,1)S(1)} collective-permute-done((bf16[64,1152]{1,0:T(8,128)(2,1)S(1)}, bf16[64,1152]{1,0:T(8,128)(2,1)S(1)}, u32[]{:S(2)}, u32[]{:S(2)}) %collective-permute-start.11) | collective-permute-done | bytes 147488 | tf_op jit(solution)/shard_map/ppermute | solution.py:212
  43.0 0.1 collective-permute-start.12
  43.1 2.6 %collective-permute-start.13 = (bf16[16,1152]{1,0:T(8,128)(2,1)S(1)}, bf16[16,1152]{1,0:T(8,128)(2,1)S(1)}, u32[]{:S(2)}, u32[]{:S(2)}) collective-permute-start(bf16[16,1152]{1,0:T(8,128)(2,1)S(1)} %get-tuple-element.63), channel_id=1, source_target_pairs={{0,8},{4,12},{8,0},{12,4},{1,9},{5,13},{9,1},{13,5},{2,10},{6,14},... | collective-permute-start | bytes 110600 | tf_op jit(solution)/shard_map/ppermute | solution.py:212
  45.7 1.7 %collective-permute-start.14 = (bf16[16,1152]{1,0:T(8,128)(2,1)S(1)}, bf16[16,1152]{1,0:T(8,128)(2,1)S(1)}, u32[]{:S(2)}, u32[]{:S(2)}) collective-permute-start(bf16[16,1152]{1,0:T(8,128)(2,1)S(1)} %get-tuple-element.64), channel_id=1, source_target_pairs={{0,12},{4,8},{8,4},{12,0},{1,13},{5,9},{9,5},{13,1},{2,14},{6,10},... | collective-permute-start | bytes 110600 | tf_op jit(solution)/shard_map/ppermute | solution.py:212
  47.4 0.0 collective-permute-done.12.refs_1_
  47.4 0.8 %collective-permute-done.13.refs_2_ = bf16[16,1152]{1,0:T(8,128)(2,1)S(1)} collective-permute-done((bf16[16,1152]{1,0:T(8,128)(2,1)S(1)}, bf16[16,1152]{1,0:T(8,128)(2,1)S(1)}, u32[]{:S(2)}, u32[]{:S(2)}) %collective-permute-start.13) | collective-permute-done | bytes 36896 | tf_op jit(solution)/shard_map/ppermute | solution.py:212
  48.2 3.3 %collective-permute-done.14.refs_3_ = bf16[16,1152]{1,0:T(8,128)(2,1)S(1)} collective-permute-done((bf16[16,1152]{1,0:T(8,128)(2,1)S(1)}, bf16[16,1152]{1,0:T(8,128)(2,1)S(1)}, u32[]{:S(2)}, u32[]{:S(2)}) %collective-permute-start.14) | collective-permute-done | bytes 36896 | tf_op jit(solution)/shard_map/ppermute | solution.py:212
  51.5 0.9 %shard_map.82 = bf16[1,64,1152]{2,1,0:T(8,128)(2,1)} custom-call(bf16[32,1152]{1,0:T(8,128)(2,1)S(1)} %get-tuple-element.50.near_ref, bf16[32,1152]{1,0:T(8,128)(2,1)S(1)} %get-tuple-element.49.refs_0_.far_ref, f32[8,1152]{1,0:T(8,128)S(1)} %get-tuple-element.41.refs_6_.mod_ref, bf16[16,1152]{1,0:T(8,128)(2,1)S(1)} %get-tuple-element.61.refs_0_, ...), custom_call_target="tpu_custom_call" | custom-call | bytes 589824 | tf_op jit(solution)/shard_map/pallas_call | solution.py:332
  (6 shorter events, 0.1 us)
Async XLA Ops:
  0.0 3.6 %collective-permute-start.1 = (bf16[64,1152]{1,0:T(8,128)(2,1)}, bf16[64,1152]{1,0:T(8,128)(2,1)S(1)}, u32[]{:S(2)}, u32[]{:S(2)}) collective-permute-start(bf16[64,1152]{1,0:T(8,128)(2,1)} %bitcast.8), channel_id=1, source_target_pairs={{0,1},{1,0},{2,3},{3,2},{4,5},{5,4},{6,7},{7,6},{8,9},{9,8},{10,11... | collective-permute-start | bytes 442376 | tf_op jit(solution)/shard_map/ppermute | solution.py:212
  0.5 7.2 %collective-permute-start = (bf16[64,1152]{1,0:T(8,128)(2,1)}, bf16[64,1152]{1,0:T(8,128)(2,1)S(1)}, u32[]{:S(2)}, u32[]{:S(2)}) collective-permute-start(bf16[64,1152]{1,0:T(8,128)(2,1)} %bitcast.9), channel_id=1, source_target_pairs={{0,2},{2,0},{1,3},{3,1},{4,6},{6,4},{5,7},{7,5},{8,10},{10,8},{9,1... | collective-permute-start | bytes 442376 | tf_op jit(solution)/shard_map/ppermute | solution.py:212
  7.7 1.4 %collective-permute-start.2 = (bf16[64,1152]{1,0:T(8,128)(2,1)S(1)}, bf16[64,1152]{1,0:T(8,128)(2,1)S(1)}, u32[]{:S(2)}, u32[]{:S(2)}) collective-permute-start(bf16[64,1152]{1,0:T(8,128)(2,1)S(1)} %collective-permute-done.refs_0_), channel_id=1, source_target_pairs={{0,1},{1,0},{2,3},{3,2},{4,5},{5,4},{6,7},{7,6},{8,9},{9,8},{10,11... | collective-permute-start | bytes 442376 | tf_op jit(solution)/shard_map/ppermute | solution.py:212
  12.1 1.6 %collective-permute-start.3 = (bf16[128,1152]{1,0:T(8,128)(2,1)S(1)}, bf16[128,1152]{1,0:T(8,128)(2,1)S(1)}, u32[]{:S(2)}, u32[]{:S(2)}) collective-permute-start(bf16[128,1152]{1,0:T(8,128)(2,1)S(1)} %get-tuple-element.43), channel_id=1, source_target_pairs={{0,1},{1,0},{2,3},{3,2},{4,5},{5,4},{6,7},{7,6},{8,9},{9,8},{10,11... | collective-permute-start | bytes 884744 | tf_op jit(solution)/shard_map/ppermute | solution.py:212
  13.8 6.8 %collective-permute-start.5 = (bf16[64,1152]{1,0:T(8,128)(2,1)S(1)}, bf16[64,1152]{1,0:T(8,128)(2,1)S(1)}, u32[]{:S(2)}, u32[]{:S(2)}) collective-permute-start(bf16[64,1152]{1,0:T(8,128)(2,1)S(1)} %get-tuple-element.48), channel_id=1, source_target_pairs={{0,2},{2,0},{1,3},{3,1},{4,6},{6,4},{5,7},{7,5},{8,10},{10,8},{9,1... | collective-permute-start | bytes 442376 | tf_op jit(solution)/shard_map/ppermute | solution.py:212
  15.7 9.5 %collective-permute-start.4 = (bf16[64,1152]{1,0:T(8,128)(2,1)S(1)}, bf16[64,1152]{1,0:T(8,128)(2,1)S(1)}, u32[]{:S(2)}, u32[]{:S(2)}) collective-permute-start(bf16[64,1152]{1,0:T(8,128)(2,1)S(1)} %get-tuple-element.45), channel_id=1, source_target_pairs={{0,2},{2,0},{1,3},{3,1},{4,6},{6,4},{5,7},{7,5},{8,10},{10,8},{9,1... | collective-permute-start | bytes 442376 | tf_op jit(solution)/shard_map/ppermute | solution.py:212
  20.9 9.8 %collective-permute-start.7 = (bf16[32,1152]{1,0:T(8,128)(2,1)S(1)}, bf16[32,1152]{1,0:T(8,128)(2,1)S(1)}, u32[]{:S(2)}, u32[]{:S(2)}) collective-permute-start(bf16[32,1152]{1,0:T(8,128)(2,1)S(1)} %get-tuple-element.53), channel_id=1, source_target_pairs={{0,8},{4,12},{8,0},{12,4},{1,9},{5,13},{9,1},{13,5},{2,10},{6,14},... | collective-permute-start | bytes 221192 | tf_op jit(solution)/shard_map/ppermute | solution.py:212
  23.8 6.9 %collective-permute-start.8 = (bf16[32,1152]{1,0:T(8,128)(2,1)S(1)}, bf16[32,1152]{1,0:T(8,128)(2,1)S(1)}, u32[]{:S(2)}, u32[]{:S(2)}) collective-permute-start(bf16[32,1152]{1,0:T(8,128)(2,1)S(1)} %get-tuple-element.54), channel_id=1, source_target_pairs={{0,12},{4,8},{8,4},{12,0},{1,13},{5,9},{9,5},{13,1},{2,14},{6,10},... | collective-permute-start | bytes 221192 | tf_op jit(solution)/shard_map/ppermute | solution.py:212
  25.4 5.2 %collective-permute-start.6 = (bf16[32,1152]{1,0:T(8,128)(2,1)S(1)}, bf16[32,1152]{1,0:T(8,128)(2,1)S(1)}, u32[]{:S(2)}, u32[]{:S(2)}) collective-permute-start(bf16[32,1152]{1,0:T(8,128)(2,1)S(1)} %get-tuple-element.52), channel_id=1, source_target_pairs={{0,4},{4,0},{8,12},{12,8},{1,5},{5,1},{9,13},{13,9},{2,6},{6,2},{1... | collective-permute-start | bytes 221192 | tf_op jit(solution)/shard_map/ppermute | solution.py:212
  30.7 1.6 %collective-permute-start.9 = (bf16[128,1152]{1,0:T(8,128)(2,1)S(1)}, bf16[128,1152]{1,0:T(8,128)(2,1)S(1)}, u32[]{:S(2)}, u32[]{:S(2)}) collective-permute-start(bf16[128,1152]{1,0:T(8,128)(2,1)S(1)} %constant_dynamic-update-slice_fusion.token_ref), channel_id=1, source_target_pairs={{0,1},{1,0},{2,3},{3,2},{4,5},{5,4},{6,7},{7,6},{8,9},{9,8},{10,11... | collective-permute-start | bytes 884744 | tf_op jit(solution)/shard_map/ppermute | solution.py:212
  35.3 1.6 %collective-permute-start.10 = (bf16[128,1152]{1,0:T(8,128)(2,1)S(1)}, bf16[128,1152]{1,0:T(8,128)(2,1)S(1)}, u32[]{:S(2)}, u32[]{:S(2)}) collective-permute-start(bf16[128,1152]{1,0:T(8,128)(2,1)S(1)} %get-tuple-element.58), channel_id=1, source_target_pairs={{0,1},{1,0},{2,3},{3,2},{4,5},{5,4},{6,7},{7,6},{8,9},{9,8},{10,11... | collective-permute-start | bytes 884744 | tf_op jit(solution)/shard_map/ppermute | solution.py:212
  37.0 6.0 %collective-permute-start.11 = (bf16[64,1152]{1,0:T(8,128)(2,1)S(1)}, bf16[64,1152]{1,0:T(8,128)(2,1)S(1)}, u32[]{:S(2)}, u32[]{:S(2)}) collective-permute-start(bf16[64,1152]{1,0:T(8,128)(2,1)S(1)} %get-tuple-element.60), channel_id=1, source_target_pairs={{0,2},{2,0},{1,3},{3,1},{4,6},{6,4},{5,7},{7,5},{8,10},{10,8},{9,1... | collective-permute-start | bytes 442376 | tf_op jit(solution)/shard_map/ppermute | solution.py:212
  43.0 4.5 %collective-permute-start.12 = (bf16[16,1152]{1,0:T(8,128)(2,1)S(1)}, bf16[16,1152]{1,0:T(8,128)(2,1)S(1)}, u32[]{:S(2)}, u32[]{:S(2)}) collective-permute-start(bf16[16,1152]{1,0:T(8,128)(2,1)S(1)} %get-tuple-element.62), channel_id=1, source_target_pairs={{0,4},{4,0},{8,12},{12,8},{1,5},{5,1},{9,13},{13,9},{2,6},{6,2},{1... | collective-permute-start | bytes 110600 | tf_op jit(solution)/shard_map/ppermute | solution.py:212
  43.1 5.1 %collective-permute-start.13 = (bf16[16,1152]{1,0:T(8,128)(2,1)S(1)}, bf16[16,1152]{1,0:T(8,128)(2,1)S(1)}, u32[]{:S(2)}, u32[]{:S(2)}) collective-permute-start(bf16[16,1152]{1,0:T(8,128)(2,1)S(1)} %get-tuple-element.63), channel_id=1, source_target_pairs={{0,8},{4,12},{8,0},{12,4},{1,9},{5,13},{9,1},{13,5},{2,10},{6,14},... | collective-permute-start | bytes 110600 | tf_op jit(solution)/shard_map/ppermute | solution.py:212
  45.7 5.8 %collective-permute-start.14 = (bf16[16,1152]{1,0:T(8,128)(2,1)S(1)}, bf16[16,1152]{1,0:T(8,128)(2,1)S(1)}, u32[]{:S(2)}, u32[]{:S(2)}) collective-permute-start(bf16[16,1152]{1,0:T(8,128)(2,1)S(1)} %get-tuple-element.64), channel_id=1, source_target_pairs={{0,12},{4,8},{8,4},{12,0},{1,13},{5,9},{9,5},{13,1},{2,14},{6,10},... | collective-permute-start | bytes 110600 | tf_op jit(solution)/shard_map/ppermute | solution.py:212
where the time goes:
time: 52.5 us; the launch traced here: 52.3 us
  waiting for transfers between devices  24.4 us (46%)
  starting transfers between devices  16.1 us (31%)
  Pallas kernels  11 us (21%)
  between operations  0.76 us (1%)
    ppermute x15, waiting for transfers between devices, exchange(): return lax.ppermute(values, axis, [(i, i ^ flip) for i in range(count)])  24.4 us
    ppermute x15, starting transfers between devices, exchange(): return lax.ppermute(values, axis, [(i, i ^ flip) for i in range(count)])  16.1 us
    pallas_call x2, Pallas kernels, block(): call(functools.partial(block_kernel, (heads, size, 2 * piece_rows if laye...  5.93 us
    pallas_call x1, Pallas kernels, body(): call(functools.partial(first_kernel, (heads, rows, piece_rows, dim)), (sh...  2.79 us
  transfers between devices with their start and end apart: 15, of which 10 were waited for; matrix products, arithmetic and copies ran while one was open for 0% of the time, Pallas kernels for 8%

commit v1 on v0

--- a/solution.py
+++ b/solution.py
@@ -8,6 +8,7 @@
 from jax.sharding import PartitionSpec as P
 
 EPSILON = 1e-06
+LOG2_E = 1.4426950408889634
 F32 = jnp.float32
 BF16 = jnp.bfloat16
 VMEM = pl.BlockSpec(memory_space=pltpu.VMEM)
@@ -39,14 +40,16 @@
     return (moved * lax.rsqrt(spread + EPSILON) * (1.0 + scale_row) + shift_row).astype(BF16)
 
 
-def shuffle(values, rows, piece_rows):
+def shuffled(ref, piece_rows):
     place = lax.axis_index("seq")
-    count = values.shape[0]
-    row = lax.broadcasted_iota(jnp.int32, (count, count), 0)
-    column = lax.broadcasted_iota(jnp.int32, (count, count), 1)
-    inside = row % rows
-    wanted = row - inside + (place ^ (inside // piece_rows)) * piece_rows + inside % piece_rows
-    return jnp.dot((wanted == column).astype(BF16), values, preferred_element_type=F32).astype(BF16)
+    rows = ref.shape[0]
+    if piece_rows % 16 == 0:
+        starts = [pl.multiple_of((place ^ k) * piece_rows, piece_rows) for k in range(rows // piece_rows)]
+        return jnp.concatenate([ref[pl.ds(start, piece_rows), :] for start in starts], axis=0)
+    row = lax.broadcasted_iota(jnp.int32, (rows, rows), 0)
+    column = lax.broadcasted_iota(jnp.int32, (rows, rows), 1)
+    wanted = (place ^ (row // piece_rows)) * piece_rows + row % piece_rows
+    return jnp.dot((wanted == column).astype(BF16), ref[...], preferred_element_type=F32).astype(BF16)
 
 
 def project(normed, weight, gain_ref, layer, heads):
@@ -65,26 +68,24 @@
 
 
 def attend(queries, keys, values, mask):
-    dim = queries.shape[0]
-    scores = lax.dot_general(keys, queries, (((0,), (0,)), ((), ())), preferred_element_type=F32)
-    weights = jnp.exp(scores * dim ** (-0.5))
+    scale = queries[0].shape[0] ** (-0.5) * LOG2_E
+    scores = [lax.dot_general(k, q, (((0,), (0,)), ((), ())), preferred_element_type=F32) for q, k in zip(queries, keys)]
+    weights = [jnp.exp2(score * scale) for score in scores]
     if mask is not None:
-        weights = weights * mask
-    total = jnp.sum(weights, axis=0, keepdims=True)
-    mixed = jnp.dot(values, weights.astype(BF16), preferred_element_type=F32)
-    return mixed / total
-
-
-def first_kernel(sizes, step_ref, table_hbm, shift_hbm, own_hbm, pair_ref, norm_hbm, qkv_hbm, out_hbm,
-                 mod_ref, gain_ref, packed_ref, own_ref, qkv0_ref, qkv1_ref, out0_ref, out1_ref,
+        weights = [weight * mask for weight in weights]
+    totals = [jnp.sum(weight, axis=0, keepdims=True) for weight in weights]
+    mixed = [jnp.dot(v, weight.astype(BF16), preferred_element_type=F32) for v, weight in zip(values, weights)]
+    return [value * (1.0 / total) for value, total in zip(mixed, totals)]
+
+
+def first_kernel(piece_rows, step_ref, table_hbm, shift_hbm, own_hbm, norm_hbm, qkv_hbm, out_hbm,
+                 mod_ref, gain_ref, normed_ref, own_ref, qkv0_ref, qkv1_ref, out0_ref, out1_ref,
                  table_ref, shift_ref, norm_ref, raw_ref, sems):
-    heads, rows, piece_rows, dim = sizes
     copies = [
         pltpu.make_async_copy(source, target, sems.at[i])
         for i, (source, target) in enumerate(
-            ((table_hbm, table_ref), (shift_hbm, shift_ref), (norm_hbm, norm_ref),
-             (own_hbm, raw_ref), (qkv_hbm.at[0], qkv0_ref),
-             (out_hbm.at[0], out0_ref), (qkv_hbm.at[1], qkv1_ref), (out_hbm.at[1], out1_ref))
+            ((table_hbm, table_ref), (shift_hbm, shift_ref), (norm_hbm, norm_ref), (own_hbm, raw_ref),
+             (qkv_hbm.at[0], qkv0_ref), (out_hbm.at[0], out0_ref), (qkv_hbm.at[1], qkv1_ref), (out_hbm.at[1], out1_ref))
         )
     ]
     for copy in copies:
@@ -96,61 +97,77 @@
         shared = table_ref[j, pl.ds(step, 1), :]
         for layer in range(2):
             mod_ref[pl.ds(3 * layer + j, 1), :] = shared + shift_ref[j, pl.ds(layer, 1), :]
+    dim = norm_ref.shape[2]
     diagonal = lax.broadcasted_iota(jnp.int32, (dim, dim), 0) == lax.broadcasted_iota(jnp.int32, (dim, dim), 1)
     for layer in range(2):
         for part in range(2):
             spread = jnp.where(diagonal, norm_ref[layer, pl.ds(part, 1), :], 0.0)
             gain_ref[2 * layer + part] = jnp.sum(spread, axis=1, keepdims=True)
-    own_ref[...] = shuffle(raw_ref[...], rows, piece_rows)
-    tokens = jnp.concatenate([raw_ref[...], pair_ref[...]], axis=0)
-    normed = layer_norm(tokens, mod_ref[pl.ds(0, 1), :], mod_ref[pl.ds(1, 1), :])
-    normed = shuffle(normed, rows, piece_rows)
-    copies[4].wait()
-    for i, piece in enumerate(project(normed, qkv0_ref[...], gain_ref, 0, heads)):
-        packed_ref[i] = piece
-    for copy in copies[5:]:
+    tokens = shuffled(raw_ref, piece_rows)
+    own_ref[...] = tokens
+    normed_ref[...] = layer_norm(tokens, mod_ref[pl.ds(0, 1), :], mod_ref[pl.ds(1, 1), :])
+    for copy in copies[4:]:
         copy.wait()
 
 
-def pair_kernel(heads, token_ref, gain_ref, qkv_ref, packed_ref):
-    for i, piece in enumerate(project(token_ref[...], qkv_ref[...], gain_ref, 1, heads)):
-        packed_ref[i] = piece
+def prepare_kernel(piece_rows, far, mod_ref, *refs):
+    theirs_ref, normed_ref = refs[far:]
+    tokens = [shuffled(ref, piece_rows) for ref in refs[:far]]
+    theirs_ref[...] = tokens[1]
+    tokens = jnp.concatenate(tokens, axis=0)
+    normed_ref[...] = layer_norm(tokens, mod_ref[pl.ds(0, 1), :], mod_ref[pl.ds(1, 1), :])
+
+
+def region(number):
+    return pl.when(lax.axis_index("seq") >= -number)
 
 
 def block_kernel(sizes, *refs):
-    heads, rows, piece_rows, sets, others, layer = sizes
-    far = refs[:others]
-    packed_ref, gain_ref, qkv_ref, out_ref = refs[others : others + 4]
-    rest = refs[others + 4 :]
-    tokens = jnp.concatenate([ref[...] for ref in far], axis=0) if others > 1 else far[0][...]
+    heads, rows, piece_rows, layer, raw, ready = sizes
+    inputs = refs[: raw + ready]
+    gain_ref, qkv_ref, out_ref = refs[raw + ready : raw + ready + 3]
+    mod_ref = refs[raw + ready + 3]
+    send_ref, keep_ref, token_ref, packed_ref, stack_ref = refs[-5:]
+    sets = token_ref.shape[0] // rows
+
     if layer == 0:
-        mod_ref, send_ref, keep_ref, theirs_ref = rest
-        theirs_ref[...] = shuffle(far[0][...], rows, piece_rows)
-        tokens = layer_norm(tokens, mod_ref[pl.ds(0, 1), :], mod_ref[pl.ds(1, 1), :])
-        tokens = shuffle(tokens, rows, piece_rows)
+        own_ref, near_ref = inputs[raw:]
+        token_ref[:rows] = own_ref[...]
+        for i in range(raw + 1):
+            token_ref[max(1, 2 * i) * rows : (max(1, 2 * i) + 1) * rows] = near_ref[i * rows : (i + 1) * rows]
+        for i in range(raw):
+            fresh = shuffled(inputs[i], piece_rows)
+            fresh = layer_norm(fresh, mod_ref[pl.ds(0, 1), :], mod_ref[pl.ds(1, 1), :])
+            token_ref[(2 * i + 3) * rows : (2 * i + 4) * rows] = fresh
     else:
-        send_ref, keep_ref = rest
-    pieces = project(tokens, qkv_ref[...], gain_ref, layer, heads)
-    everything = [jnp.concatenate([packed_ref[i], pieces[i]], axis=1) for i in range(3 * heads)]
-    attended = []
-    if layer == 0:
-        for head in range(heads):
-            attended.append(attend(*everything[3 * head : 3 * head + 3], None))
-    else:
-        key = lax.broadcasted_iota(jnp.int32, (rows, rows), 0)
-        query = lax.broadcasted_iota(jnp.int32, (rows, rows), 1)
-        mask = (key % piece_rows == query % piece_rows).astype(F32)
-        for head in range(heads):
-            parts = []
-            for start in range(0, sets * rows, rows):
-                cut = [value[:, start : start + rows] for value in everything[3 * head : 3 * head + 3]]
-                parts.append(attend(*cut, mask))
-            attended.append(jnp.concatenate(parts, axis=1))
-    stacked = jnp.concatenate(attended, axis=0).astype(BF16)
-    partial = lax.dot_general(stacked, out_ref[...], (((0,), (0,)), ((), ())), preferred_element_type=F32)
-    for i in range(sets // 2):
-        keep_ref[i * rows : (i + 1) * rows] = partial[2 * i * rows : (2 * i + 1) * rows]
-        send_ref[i * rows : (i + 1) * rows] = partial[(2 * i + 1) * rows : (2 * i + 2) * rows].astype(BF16)
+        for i, ref in enumerate(inputs):
+            token_ref[i * rows : (i + 1) * rows] = ref[...]
+
+    @region(1)
+    def _():
+        for i, piece in enumerate(project(token_ref[...], qkv_ref[...], gain_ref, layer, heads)):
+            packed_ref[i] = piece
+
+    @region(2)
+    def _():
+        dim = packed_ref.shape[1]
+        span = token_ref.shape[0] if layer == 0 else rows
+        mask = None
+        if layer:
+            key = lax.broadcasted_iota(jnp.int32, (rows, rows), 0)
+            query = lax.broadcasted_iota(jnp.int32, (rows, rows), 1)
+            mask = (key % piece_rows == query % piece_rows).astype(F32)
+        places = [(head, start) for start in range(0, token_ref.shape[0], span) for head in range(heads)]
+        cut = [[packed_ref[3 * head + part, :, start : start + span] for head, start in places] for part in range(3)]
+        for (head, start), value in zip(places, attend(*cut, mask)):
+            stack_ref[head * dim : (head + 1) * dim, start : start + span] = value.astype(BF16)
+
+    @region(3)
+    def _():
+        partial = lax.dot_general(stack_ref[...], out_ref[...], (((0,), (0,)), ((), ())), preferred_element_type=F32)
+        for i in range(sets // 2):
+            keep_ref[i * rows : (i + 1) * rows] = partial[2 * i * rows : (2 * i + 1) * rows]
+            send_ref[i * rows : (i + 1) * rows] = partial[(2 * i + 1) * rows : (2 * i + 2) * rows].astype(BF16)
 
 
 def fold_kernel(keep_ref, got_ref, send_ref, kept_ref):
@@ -205,7 +222,9 @@
     update = jnp.concatenate([ref[...] for ref in refs[:pieces]], axis=0).astype(F32)
     current = jnp.concatenate([near_ref[...], far_ref[...]], axis=0).astype(F32)
     mixed = (current + mod_ref[pl.ds(5, 1), :] * update).astype(BF16)
-    refs[pieces][0] = shuffle(mixed, mixed.shape[0], mixed.shape[0] // pieces)
+    out_ref, mixed_ref = refs[pieces:]
+    mixed_ref[...] = mixed
+    out_ref[0] = shuffled(mixed_ref, mixed.shape[0] // pieces)
 
 
 def exchange(values, axis, count, flip):
@@ -240,44 +259,49 @@
             got = exchange(send, "head", head_count, flip)
         return keep, got
 
-    def block(layer, packed, others, qkv, out, extra):
-        size = others[0].shape[0]
-        sets = blocks * rows // size
+    def block(layer, raw, ready, qkv, out, extra):
         half = blocks // 2 * rows
-        outputs = (shape((half, width), BF16), shape((half, width), F32))
-        if layer == 0:
-            outputs += (shape((rows, width), BF16),)
         return call(
-            functools.partial(block_kernel, (heads, size, 2 * piece_rows if layer else piece_rows, sets, len(others), layer)),
-            outputs,
-            [VMEM] * (len(others) + 4 + len(extra)),
-            flops=2 * len(others) * size * heads * triple * width + 2 * blocks * rows * depth * width,
+            functools.partial(
+                block_kernel,
+                (heads, 2 * rows if layer else rows, 2 * piece_rows if layer else piece_rows, layer, len(raw), len(ready)),
+            ),
+            (shape((half, width), BF16), shape((half, width), F32)),
+            [VMEM] * (len(raw) + len(ready) + 3 + len(extra)),
+            [pltpu.VMEM((blocks * rows, width), BF16), pltpu.VMEM((3 * heads, dim, blocks * rows), BF16),
+             pltpu.VMEM((depth, blocks * rows), BF16)],
+            flops=2 * blocks * rows * (heads * triple + depth) * width,
             moved=qkv.size * 2,
-        )(*others, packed, gains, qkv, out, *extra)
+        )(*raw, *ready, gains, qkv, out, *extra)
 
     qkv = qkv_weight.transpose(0, 2, 3, 1).reshape(2, heads * triple, width)
     table = time_table.transpose(1, 0, 2)
     shift = shift_table.transpose(1, 0, 2)
-    packed_shape = shape((3 * heads, dim, 2 * rows), BF16)
-    work = 2 * 2 * rows * heads * triple * width
 
     held = spread(own, flips)
     pair = exchange(own, "sub", sub_count, 1)
-    mods, gains, packed, mine, qkv0, qkv1, out0, out1 = call(
-        functools.partial(first_kernel, (heads, rows, piece_rows, dim)),
-        (shape((8, width), F32), shape((4, dim, 1), F32), packed_shape, shape((rows, width), BF16),
+    mods, gains, normed, mine, qkv0, qkv1, out0, out1 = call(
+        functools.partial(first_kernel, piece_rows),
+        (shape((8, width), F32), shape((4, dim, 1), F32), shape((rows, width), BF16), shape((rows, width), BF16),
          shape(qkv.shape[1:], BF16), shape(qkv.shape[1:], BF16), shape((depth, width), BF16), shape((depth, width), BF16)),
-        [SMEM, HBM, HBM, HBM, VMEM, HBM, HBM, HBM],
+        [SMEM] + [HBM] * 6,
         [pltpu.VMEM(table.shape, F32), pltpu.VMEM(shift.shape, F32),
          pltpu.VMEM(norm_gains.shape, F32), pltpu.VMEM(own.shape, BF16), pltpu.SemaphoreType.DMA((8,))],
-        flops=work,
+        flops=10**9,
         moved=qkv.size * 2,
-    )(timestep, in_hbm(table), in_hbm(shift), in_hbm(own), pair, in_hbm(norm_gains), in_hbm(qkv), in_hbm(out_weight))
+    )(timestep, in_hbm(table), in_hbm(shift), in_hbm(own), in_hbm(norm_gains), in_hbm(qkv), in_hbm(out_weight))
 
     far = [held[j] for j in sorted(held) if j]
-    far, packed = lax.optimization_barrier((far, packed))
-    others = [v for value in far for v in (value, exchange(value, "sub", sub_count, 1))]
-    send, keep, theirs = block(0, packed, others, qkv0, out0, [mods])
+    far, mods = lax.optimization_barrier((far, mods))
+    fresh = [exchange(value, "sub", sub_count, 1) for value in far]
+    theirs, near = call(
+        functools.partial(prepare_kernel, piece_rows, 1 + len(far)),
+        (shape((rows, width), BF16), shape(((1 + len(far)) * rows, width), BF16)),
+        [VMEM] * (2 + len(far)),
+        flops=5 * 10**8,
+        moved=rows * width * 8,
+    )(mods, pair, *far)
+    send, keep = block(0, fresh, [normed, near], qkv0, out0, [mods])
 
     keep, got = reduce(send, keep, flips[1:])
     near, distant, kept = call(
@@ -308,10 +332,7 @@
     held = spread(tokens, flips[1:])
     for j in list(held):
         held[j | 1] = exchange(held[j], "sub", sub_count, 1)
-    packed = call(
-        functools.partial(pair_kernel, heads), packed_shape, [VMEM] * 3, flops=work, moved=qkv.size
-    )(tokens, gains, qkv1)
-    send, keep = block(1, packed, [held[j] for j in sorted(held) if j], qkv1, out1, [])
+    send, keep = block(1, [], [held[j] for j in sorted(held)], qkv1, out1, [])
 
     keep, got = reduce(send, keep, flips[1:])
     send, keep = call(
@@ -333,6 +354,7 @@
         functools.partial(last_kernel, seq_count),
         jax.ShapeDtypeStruct((1, rows, width), BF16),
         [VMEM] * (3 + seq_count),
+        [pltpu.VMEM((rows, width), BF16)],
         moved=rows * width * 8,
     )(current_near, current_far, mods, *[back[k] for k in range(seq_count)])
 

time: 52.5 us -> 49.6 us (0.945)
  Pallas kernels: 11 us -> 8.35 us
    pallas_call x4, Pallas kernels: 9.42 us -> 6.92 us  [the longest x2 3.84 us: block(): call(functools.partial(block_kernel, (heads, 2 * rows if layer else rows,...]
  transfers between devices with their start and end apart: 15 -> 15, of which waited for: 10 -> 10; matrix products, arithmetic and copies ran while one was open for 0% -> 0% of each run, Pallas kernels for 8% -> 7%
where the time goes in v1:
time: 49.6 us; the launch traced here: 49.5 us
  waiting for transfers between devices  24.2 us (49%)
  starting transfers between devices  16.1 us (32%)
  Pallas kernels  8.35 us (17%)
  between operations  0.76 us (2%)
    ppermute x15, waiting for transfers between devices, exchange(): return lax.ppermute(values, axis, [(i, i ^ flip) for i in range(count)])  24.2 us
    ppermute x15, starting transfers between devices, exchange(): return lax.ppermute(values, axis, [(i, i ^ flip) for i in range(count)])  16.1 us
    pallas_call x2, Pallas kernels, block(): call(functools.partial(block_kernel, (heads, 2 * rows if layer else rows,...  3.84 us
    pallas_call x1, Pallas kernels, body(): call(functools.partial(first_kernel, piece_rows), (shape((8, width), F32)...  2.79 us
  transfers between devices with their start and end apart: 15, of which 10 were waited for; matrix products, arithmetic and copies ran while one was open for 0% of the time, Pallas kernels for 7%

profile of v1, /device:TPU:0, one launch (start us, length us, event | category | flops | bytes accessed | tf_op | source)
XLA Modules:
  0.0 49.5 jit_solution(17563023915653081414)
XLA Ops:
  0.0 3.0 %collective-permute-start = (bf16[64,1152]{1,0:T(8,128)(2,1)}, bf16[64,1152]{1,0:T(8,128)(2,1)S(1)}, u32[]{:S(2)}, u32[]{:S(2)}) collective-permute-start(bf16[64,1152]{1,0:T(8,128)(2,1)} %bitcast.8), channel_id=1, source_target_pairs={{0,2},{2,0},{1,3},{3,1},{4,6},{6,4},{5,7},{7,5},{8,10},{10,8},{9,1... | collective-permute-start | bytes 442376 | tf_op jit(solution)/shard_map/ppermute | solution.py:231
  3.0 0.0 collective-permute-start.2
  3.6 2.8 %shard_map.73 = (f32[8,1152]{1,0:T(8,128)S(1)}, f32[4,72,1]{2,1,0:T(8,128)S(1)}, bf16[64,1152]{1,0:T(8,128)(2,1)S(1)}, bf16[64,1152]{1,0:T(8,128)(2,1)S(1)}, bf1...) custom-call(s32[1]{0:T(128)S(6)} %copy.11.step_ref, ...), custom_call_target="tpu_custom_call" | custom-call | flops 1000000000 | bytes 3981312 | tf_op jit(solution)/shard_map/pallas_call | solution.py:283
  6.4 0.6 %collective-permute-done.refs_1_ = bf16[64,1152]{1,0:T(8,128)(2,1)S(1)} collective-permute-done((bf16[64,1152]{1,0:T(8,128)(2,1)}, bf16[64,1152]{1,0:T(8,128)(2,1)S(1)}, u32[]{:S(2)}, u32[]{:S(2)}) %collective-permute-start) | collective-permute-done | bytes 147488 | tf_op jit(solution)/shard_map/ppermute | solution.py:231
  7.0 0.0 collective-permute-start.1
  7.0 0.0 collective-permute-done.2.refs_0_
  7.0 0.3 shard_map.74
  7.3 1.1 %collective-permute-done.1.refs_0_ = bf16[64,1152]{1,0:T(8,128)(2,1)S(1)} collective-permute-done((bf16[64,1152]{1,0:T(8,128)(2,1)S(1)}, bf16[64,1152]{1,0:T(8,128)(2,1)S(1)}, u32[]{:S(2)}, u32[]{:S(2)}) %collective-permute-start.1) | collective-permute-done | bytes 147488 | tf_op jit(solution)/shard_map/ppermute | solution.py:231
  8.4 2.0 %shard_map.75 = (bf16[128,1152]{1,0:T(8,128)(2,1)S(1)}, f32[128,1152]{1,0:T(8,128)S(1)}) custom-call(bf16[64,1152]{1,0:T(8,128)(2,1)S(1)} %collective-permute-done.1.refs_0_, bf16[64,1152]{1,0:T(8,128)(2,1)S(1)} %get-tuple-element.38.refs_1_, bf16[128,1152]{1,0:T(8,128)(2,1)S(1)} %get-tuple-element.40.refs_2_, ...), custom_call_target="tpu_custom_call" | custom-call | flops 679477248 | bytes 1990656 | tf_op jit(solution)/shard_map/pallas_call | solution.py:264
  10.4 0.2 collective-permute-start.3
  10.7 1.4 %collective-permute-done.3.got_ref = bf16[128,1152]{1,0:T(8,128)(2,1)S(1)} collective-permute-done((bf16[128,1152]{1,0:T(8,128)(2,1)S(1)}, bf16[128,1152]{1,0:T(8,128)(2,1)S(1)}, u32[]{:S(2)}, u32[]{:S(2)}) %collective-permute-start.3) | collective-permute-done | bytes 294944 | tf_op jit(solution)/shard_map/ppermute | solution.py:231
  12.1 0.1 shard_map.76
  12.2 1.8 %collective-permute-start.5 = (bf16[64,1152]{1,0:T(8,128)(2,1)S(1)}, bf16[64,1152]{1,0:T(8,128)(2,1)S(1)}, u32[]{:S(2)}, u32[]{:S(2)}) collective-permute-start(bf16[64,1152]{1,0:T(8,128)(2,1)S(1)} %get-tuple-element.50), channel_id=1, source_target_pairs={{0,2},{2,0},{1,3},{3,1},{4,6},{6,4},{5,7},{7,5},{8,10},{10,8},{9,1... | collective-permute-start | bytes 442376 | tf_op jit(solution)/shard_map/ppermute | solution.py:231
  14.0 0.3 collective-permute-start.4
  14.3 4.7 %collective-permute-done.5.got_ref = bf16[64,1152]{1,0:T(8,128)(2,1)S(1)} collective-permute-done((bf16[64,1152]{1,0:T(8,128)(2,1)S(1)}, bf16[64,1152]{1,0:T(8,128)(2,1)S(1)}, u32[]{:S(2)}, u32[]{:S(2)}) %collective-permute-start.5) | collective-permute-done | bytes 147488 | tf_op jit(solution)/shard_map/ppermute | solution.py:231
  19.0 0.3 shard_map.77
  19.3 2.9 %collective-permute-start.7 = (bf16[32,1152]{1,0:T(8,128)(2,1)S(1)}, bf16[32,1152]{1,0:T(8,128)(2,1)S(1)}, u32[]{:S(2)}, u32[]{:S(2)}) collective-permute-start(bf16[32,1152]{1,0:T(8,128)(2,1)S(1)} %get-tuple-element.55), channel_id=1, source_target_pairs={{0,8},{4,12},{8,0},{12,4},{1,9},{5,13},{9,1},{13,5},{2,10},{6,14},... | collective-permute-start | bytes 221192 | tf_op jit(solution)/shard_map/ppermute | solution.py:231
  22.2 1.4 %collective-permute-start.8 = (bf16[32,1152]{1,0:T(8,128)(2,1)S(1)}, bf16[32,1152]{1,0:T(8,128)(2,1)S(1)}, u32[]{:S(2)}, u32[]{:S(2)}) collective-permute-start(bf16[32,1152]{1,0:T(8,128)(2,1)S(1)} %get-tuple-element.56), channel_id=1, source_target_pairs={{0,12},{4,8},{8,4},{12,0},{1,13},{5,9},{9,5},{13,1},{2,14},{6,10},... | collective-permute-start | bytes 221192 | tf_op jit(solution)/shard_map/ppermute | solution.py:231
  23.5 0.0 collective-permute-done.4.got_ref
  23.5 0.3 shard_map.78
  23.8 0.3 collective-permute-start.6
  24.1 4.9 %collective-permute-done.6 = bf16[32,1152]{1,0:T(8,128)(2,1)S(1)} collective-permute-done((bf16[32,1152]{1,0:T(8,128)(2,1)S(1)}, bf16[32,1152]{1,0:T(8,128)(2,1)S(1)}, u32[]{:S(2)}, u32[]{:S(2)}) %collective-permute-start.6) | collective-permute-done | bytes 73760 | tf_op jit(solution)/shard_map/ppermute | solution.py:231
  29.0 0.0 collective-permute-done.7
  29.0 0.0 collective-permute-done.8
  29.1 0.1 collective-permute-start.9
  29.1 1.6 %collective-permute-done.9.refs_1_ = bf16[128,1152]{1,0:T(8,128)(2,1)S(1)} collective-permute-done((bf16[128,1152]{1,0:T(8,128)(2,1)S(1)}, bf16[128,1152]{1,0:T(8,128)(2,1)S(1)}, u32[]{:S(2)}, u32[]{:S(2)}) %collective-permute-start.9) | collective-permute-done | bytes 294944 | tf_op jit(solution)/shard_map/ppermute | solution.py:231
  30.7 1.8 %shard_map.79 = (bf16[128,1152]{1,0:T(8,128)(2,1)S(1)}, f32[128,1152]{1,0:T(8,128)S(1)}) custom-call(bf16[128,1152]{1,0:T(8,128)(2,1)S(1)} %constant_dynamic-update-slice_fusion.refs_0_, bf16[128,1152]{1,0:T(8,128)(2,1)S(1)} %collective-permute-done.9.refs_1_, f32[4,72,1]{2,1,0:T(8,128)S(1)} %get-tuple-element.41.refs_3_.refs_2_, ...), custom_call_target="tpu_custom_call" | custom-call | flops 679477248 | bytes 1990656 | tf_op jit(solution)/shard_map/pallas_call | solution.py:264
  32.5 0.2 collective-permute-start.10
  32.7 1.4 %collective-permute-done.10.got_ref = bf16[128,1152]{1,0:T(8,128)(2,1)S(1)} collective-permute-done((bf16[128,1152]{1,0:T(8,128)(2,1)S(1)}, bf16[128,1152]{1,0:T(8,128)(2,1)S(1)}, u32[]{:S(2)}, u32[]{:S(2)}) %collective-permute-start.10) | collective-permute-done | bytes 294944 | tf_op jit(solution)/shard_map/ppermute | solution.py:231
  34.2 1.5 %collective-permute-start.11 = (bf16[64,1152]{1,0:T(8,128)(2,1)S(1)}, bf16[64,1152]{1,0:T(8,128)(2,1)S(1)}, u32[]{:S(2)}, u32[]{:S(2)}) collective-permute-start(bf16[64,1152]{1,0:T(8,128)(2,1)S(1)} %get-tuple-element.62), channel_id=1, source_target_pairs={{0,2},{2,0},{1,3},{3,1},{4,6},{6,4},{5,7},{7,5},{8,10},{10,8},{9,1... | collective-permute-start | bytes 442376 | tf_op jit(solution)/shard_map/ppermute | solution.py:231
  35.8 4.4 %collective-permute-done.11.got_ref = bf16[64,1152]{1,0:T(8,128)(2,1)S(1)} collective-permute-done((bf16[64,1152]{1,0:T(8,128)(2,1)S(1)}, bf16[64,1152]{1,0:T(8,128)(2,1)S(1)}, u32[]{:S(2)}, u32[]{:S(2)}) %collective-permute-start.11) | collective-permute-done | bytes 147488 | tf_op jit(solution)/shard_map/ppermute | solution.py:231
  40.2 0.1 collective-permute-start.12
  40.3 2.7 %collective-permute-start.13 = (bf16[16,1152]{1,0:T(8,128)(2,1)S(1)}, bf16[16,1152]{1,0:T(8,128)(2,1)S(1)}, u32[]{:S(2)}, u32[]{:S(2)}) collective-permute-start(bf16[16,1152]{1,0:T(8,128)(2,1)S(1)} %get-tuple-element.65), channel_id=1, source_target_pairs={{0,8},{4,12},{8,0},{12,4},{1,9},{5,13},{9,1},{13,5},{2,10},{6,14},... | collective-permute-start | bytes 110600 | tf_op jit(solution)/shard_map/ppermute | solution.py:231
  43.0 1.7 %collective-permute-start.14 = (bf16[16,1152]{1,0:T(8,128)(2,1)S(1)}, bf16[16,1152]{1,0:T(8,128)(2,1)S(1)}, u32[]{:S(2)}, u32[]{:S(2)}) collective-permute-start(bf16[16,1152]{1,0:T(8,128)(2,1)S(1)} %get-tuple-element.66), channel_id=1, source_target_pairs={{0,12},{4,8},{8,4},{12,0},{1,13},{5,9},{9,5},{13,1},{2,14},{6,10},... | collective-permute-start | bytes 110600 | tf_op jit(solution)/shard_map/ppermute | solution.py:231
  44.7 0.0 collective-permute-done.12.refs_1_
  44.7 0.8 %collective-permute-done.13.refs_2_ = bf16[16,1152]{1,0:T(8,128)(2,1)S(1)} collective-permute-done((bf16[16,1152]{1,0:T(8,128)(2,1)S(1)}, bf16[16,1152]{1,0:T(8,128)(2,1)S(1)}, u32[]{:S(2)}, u32[]{:S(2)}) %collective-permute-start.13) | collective-permute-done | bytes 36896 | tf_op jit(solution)/shard_map/ppermute | solution.py:231
  45.4 3.3 %collective-permute-done.14.refs_3_ = bf16[16,1152]{1,0:T(8,128)(2,1)S(1)} collective-permute-done((bf16[16,1152]{1,0:T(8,128)(2,1)S(1)}, bf16[16,1152]{1,0:T(8,128)(2,1)S(1)}, u32[]{:S(2)}, u32[]{:S(2)}) %collective-permute-start.14) | collective-permute-done | bytes 36896 | tf_op jit(solution)/shard_map/ppermute | solution.py:231
  48.7 0.7 %shard_map.82 = bf16[1,64,1152]{2,1,0:T(8,128)(2,1)} custom-call(bf16[32,1152]{1,0:T(8,128)(2,1)S(1)} %get-tuple-element.52.near_ref, bf16[32,1152]{1,0:T(8,128)(2,1)S(1)} %get-tuple-element.51.refs_0_.far_ref, f32[8,1152]{1,0:T(8,128)S(1)} %get-tuple-element.39.mod_ref.refs_6_, bf16[16,1152]{1,0:T(8,128)(2,1)S(1)} %get-tuple-element.63.refs_0_, ...), custom_call_target="tpu_custom_call" | custom-call | bytes 589824 | tf_op jit(solution)/shard_map/pallas_call | solution.py:353
  (6 shorter events, 0.1 us)
Async XLA Ops:
  0.0 7.0 %collective-permute-start = (bf16[64,1152]{1,0:T(8,128)(2,1)}, bf16[64,1152]{1,0:T(8,128)(2,1)S(1)}, u32[]{:S(2)}, u32[]{:S(2)}) collective-permute-start(bf16[64,1152]{1,0:T(8,128)(2,1)} %bitcast.8), channel_id=1, source_target_pairs={{0,2},{2,0},{1,3},{3,1},{4,6},{6,4},{5,7},{7,5},{8,10},{10,8},{9,1... | collective-permute-start | bytes 442376 | tf_op jit(solution)/shard_map/ppermute | solution.py:231
  3.0 4.1 %collective-permute-start.2 = (bf16[64,1152]{1,0:T(8,128)(2,1)}, bf16[64,1152]{1,0:T(8,128)(2,1)S(1)}, u32[]{:S(2)}, u32[]{:S(2)}) collective-permute-start(bf16[64,1152]{1,0:T(8,128)(2,1)} %bitcast.9), channel_id=1, source_target_pairs={{0,1},{1,0},{2,3},{3,2},{4,5},{5,4},{6,7},{7,6},{8,9},{9,8},{10,11... | collective-permute-start | bytes 442376 | tf_op jit(solution)/shard_map/ppermute | solution.py:231
  7.0 1.4 %collective-permute-start.1 = (bf16[64,1152]{1,0:T(8,128)(2,1)S(1)}, bf16[64,1152]{1,0:T(8,128)(2,1)S(1)}, u32[]{:S(2)}, u32[]{:S(2)}) collective-permute-start(bf16[64,1152]{1,0:T(8,128)(2,1)S(1)} %collective-permute-done.refs_1_), channel_id=1, source_target_pairs={{0,1},{1,0},{2,3},{3,2},{4,5},{5,4},{6,7},{7,6},{8,9},{9,8},{10,11... | collective-permute-start | bytes 442376 | tf_op jit(solution)/shard_map/ppermute | solution.py:231
  10.4 1.6 %collective-permute-start.3 = (bf16[128,1152]{1,0:T(8,128)(2,1)S(1)}, bf16[128,1152]{1,0:T(8,128)(2,1)S(1)}, u32[]{:S(2)}, u32[]{:S(2)}) collective-permute-start(bf16[128,1152]{1,0:T(8,128)(2,1)S(1)} %get-tuple-element.45), channel_id=1, source_target_pairs={{0,1},{1,0},{2,3},{3,2},{4,5},{5,4},{6,7},{7,6},{8,9},{9,8},{10,11... | collective-permute-start | bytes 884744 | tf_op jit(solution)/shard_map/ppermute | solution.py:231
  12.2 6.8 %collective-permute-start.5 = (bf16[64,1152]{1,0:T(8,128)(2,1)S(1)}, bf16[64,1152]{1,0:T(8,128)(2,1)S(1)}, u32[]{:S(2)}, u32[]{:S(2)}) collective-permute-start(bf16[64,1152]{1,0:T(8,128)(2,1)S(1)} %get-tuple-element.50), channel_id=1, source_target_pairs={{0,2},{2,0},{1,3},{3,1},{4,6},{6,4},{5,7},{7,5},{8,10},{10,8},{9,1... | collective-permute-start | bytes 442376 | tf_op jit(solution)/shard_map/ppermute | solution.py:231
  14.0 9.5 %collective-permute-start.4 = (bf16[64,1152]{1,0:T(8,128)(2,1)S(1)}, bf16[64,1152]{1,0:T(8,128)(2,1)S(1)}, u32[]{:S(2)}, u32[]{:S(2)}) collective-permute-start(bf16[64,1152]{1,0:T(8,128)(2,1)S(1)} %get-tuple-element.47), channel_id=1, source_target_pairs={{0,2},{2,0},{1,3},{3,1},{4,6},{6,4},{5,7},{7,5},{8,10},{10,8},{9,1... | collective-permute-start | bytes 442376 | tf_op jit(solution)/shard_map/ppermute | solution.py:231
  19.3 9.8 %collective-permute-start.7 = (bf16[32,1152]{1,0:T(8,128)(2,1)S(1)}, bf16[32,1152]{1,0:T(8,128)(2,1)S(1)}, u32[]{:S(2)}, u32[]{:S(2)}) collective-permute-start(bf16[32,1152]{1,0:T(8,128)(2,1)S(1)} %get-tuple-element.55), channel_id=1, source_target_pairs={{0,8},{4,12},{8,0},{12,4},{1,9},{5,13},{9,1},{13,5},{2,10},{6,14},... | collective-permute-start | bytes 221192 | tf_op jit(solution)/shard_map/ppermute | solution.py:231
  22.2 6.9 %collective-permute-start.8 = (bf16[32,1152]{1,0:T(8,128)(2,1)S(1)}, bf16[32,1152]{1,0:T(8,128)(2,1)S(1)}, u32[]{:S(2)}, u32[]{:S(2)}) collective-permute-start(bf16[32,1152]{1,0:T(8,128)(2,1)S(1)} %get-tuple-element.56), channel_id=1, source_target_pairs={{0,12},{4,8},{8,4},{12,0},{1,13},{5,9},{9,5},{13,1},{2,14},{6,10},... | collective-permute-start | bytes 221192 | tf_op jit(solution)/shard_map/ppermute | solution.py:231
  23.8 5.2 %collective-permute-start.6 = (bf16[32,1152]{1,0:T(8,128)(2,1)S(1)}, bf16[32,1152]{1,0:T(8,128)(2,1)S(1)}, u32[]{:S(2)}, u32[]{:S(2)}) collective-permute-start(bf16[32,1152]{1,0:T(8,128)(2,1)S(1)} %get-tuple-element.54), channel_id=1, source_target_pairs={{0,4},{4,0},{8,12},{12,8},{1,5},{5,1},{9,13},{13,9},{2,6},{6,2},{1... | collective-permute-start | bytes 221192 | tf_op jit(solution)/shard_map/ppermute | solution.py:231
  29.1 1.6 %collective-permute-start.9 = (bf16[128,1152]{1,0:T(8,128)(2,1)S(1)}, bf16[128,1152]{1,0:T(8,128)(2,1)S(1)}, u32[]{:S(2)}, u32[]{:S(2)}) collective-permute-start(bf16[128,1152]{1,0:T(8,128)(2,1)S(1)} %constant_dynamic-update-slice_fusion.refs_0_), channel_id=1, source_target_pairs={{0,1},{1,0},{2,3},{3,2},{4,5},{5,4},{6,7},{7,6},{8,9},{9,8},{10,11... | collective-permute-start | bytes 884744 | tf_op jit(solution)/shard_map/ppermute | solution.py:231
  32.5 1.6 %collective-permute-start.10 = (bf16[128,1152]{1,0:T(8,128)(2,1)S(1)}, bf16[128,1152]{1,0:T(8,128)(2,1)S(1)}, u32[]{:S(2)}, u32[]{:S(2)}) collective-permute-start(bf16[128,1152]{1,0:T(8,128)(2,1)S(1)} %get-tuple-element.60), channel_id=1, source_target_pairs={{0,1},{1,0},{2,3},{3,2},{4,5},{5,4},{6,7},{7,6},{8,9},{9,8},{10,11... | collective-permute-start | bytes 884744 | tf_op jit(solution)/shard_map/ppermute | solution.py:231
  34.2 6.0 %collective-permute-start.11 = (bf16[64,1152]{1,0:T(8,128)(2,1)S(1)}, bf16[64,1152]{1,0:T(8,128)(2,1)S(1)}, u32[]{:S(2)}, u32[]{:S(2)}) collective-permute-start(bf16[64,1152]{1,0:T(8,128)(2,1)S(1)} %get-tuple-element.62), channel_id=1, source_target_pairs={{0,2},{2,0},{1,3},{3,1},{4,6},{6,4},{5,7},{7,5},{8,10},{10,8},{9,1... | collective-permute-start | bytes 442376 | tf_op jit(solution)/shard_map/ppermute | solution.py:231
  40.2 4.5 %collective-permute-start.12 = (bf16[16,1152]{1,0:T(8,128)(2,1)S(1)}, bf16[16,1152]{1,0:T(8,128)(2,1)S(1)}, u32[]{:S(2)}, u32[]{:S(2)}) collective-permute-start(bf16[16,1152]{1,0:T(8,128)(2,1)S(1)} %get-tuple-element.64), channel_id=1, source_target_pairs={{0,4},{4,0},{8,12},{12,8},{1,5},{5,1},{9,13},{13,9},{2,6},{6,2},{1... | collective-permute-start | bytes 110600 | tf_op jit(solution)/shard_map/ppermute | solution.py:231
  40.3 5.1 %collective-permute-start.13 = (bf16[16,1152]{1,0:T(8,128)(2,1)S(1)}, bf16[16,1152]{1,0:T(8,128)(2,1)S(1)}, u32[]{:S(2)}, u32[]{:S(2)}) collective-permute-start(bf16[16,1152]{1,0:T(8,128)(2,1)S(1)} %get-tuple-element.65), channel_id=1, source_target_pairs={{0,8},{4,12},{8,0},{12,4},{1,9},{5,13},{9,1},{13,5},{2,10},{6,14},... | collective-permute-start | bytes 110600 | tf_op jit(solution)/shard_map/ppermute | solution.py:231
  43.0 5.8 %collective-permute-start.14 = (bf16[16,1152]{1,0:T(8,128)(2,1)S(1)}, bf16[16,1152]{1,0:T(8,128)(2,1)S(1)}, u32[]{:S(2)}, u32[]{:S(2)}) collective-permute-start(bf16[16,1152]{1,0:T(8,128)(2,1)S(1)} %get-tuple-element.66), channel_id=1, source_target_pairs={{0,12},{4,8},{8,4},{12,0},{1,13},{5,9},{9,5},{13,1},{2,14},{6,10},... | collective-permute-start | bytes 110600 | tf_op jit(solution)/shard_map/ppermute | solution.py:231
